TPU v7x, 32 devices: a whole 2x2x4 slice. The times are simulated.
32 devices in a mesh: nx: 4 (over x, core), ny: 4 (over z), img: 2 (over y).
Axes of the slice: x: 2, y: 2, z: 4, core: 2. Of those that a mesh axis runs over, the one named last changes fastest.
Arguments:
- features: bfloat16 [256, 8192], P(('nx', 'ny', 'img')), may hold values from 0 to 2
- link_weight: bfloat16 [3, 16, 16, 128, 128], P(None, ('nx', 'ny')), may hold values from -0.5 to 0.5
- link_row: int32 [3, 16, 16], P(None, ('nx', 'ny')), may hold values from 0 to 3
- link_col: int32 [3, 16, 16], P(None, None, ('nx', 'ny')), may hold values from 0 to 3
- link_live: int32 [3, 16, 16], P(None, ('nx', 'ny')), may hold values from 0 to 1, as said below
- bias: float32 [3, 8192], P(None, ('nx', 'ny')), may hold values from -3 to 3
Outputs:
- activations: bfloat16 [256, 8192], P(('nx', 'ny', 'img'))
Inputs may be any that keep to these rules, and one draw needn't show every extreme that they name: `link_live`: in every layer at most 12 of the links of one source device are live, and exactly 12 for some source device.
All inputs are finite; a program needn't handle non-finite values.
Results may differ from a plain program's by a relative error of at most 0.0072.
Values may be sent and summed in bfloat16 or wider, within the bound.
A program may use at most 64 MiB of HBM per device.

v0:
```python
import functools

import jax
import jax.numpy as jnp
from jax import lax
from jax.experimental import pallas as pl
from jax.experimental.pallas import tpu as pltpu
from jax.sharding import PartitionSpec as P

MESH = pl.DeviceIdType.MESH
CHUNKS = 2


def combine_links(received, col_ids, width):
    onehot = (col_ids[:, None] == jnp.arange(width, dtype=jnp.int32)[None, :]).astype(jnp.bfloat16)
    summed = jnp.einsum("dq,dis->iqs", onehot, received, preferred_element_type=jnp.float32)
    return summed.reshape(summed.shape[0], width * received.shape[2])


def link_products(blocks, weights, row_ids, live_mask):
    masked = weights * live_mask.astype(jnp.bfloat16)[:, None, None]
    gathered = jnp.take(blocks, row_ids, axis=1)
    result = jnp.einsum(
        "ier,ers->eis", gathered, masked, preferred_element_type=jnp.float32
    ).astype(jnp.bfloat16)
    return result


def local(features, link_weight, link_row, link_col, link_live, bias):
    block_size = link_weight.shape[-1]
    width = bias.shape[1] // block_size
    hidden = lax.all_to_all(features, ("nx", "ny"), split_axis=1, concat_axis=0, tiled=True)
    image_rows = hidden.shape[0]
    for layer_idx in range(bias.shape[0]):
        blocks = hidden.reshape(image_rows, width, block_size)
        link_terms = link_products(
            blocks, link_weight[layer_idx, 0], link_row[layer_idx, 0], link_live[layer_idx, 0]
        )
        col_ids = link_col[layer_idx, :, 0]
        summed = combine_links(
            lax.all_to_all(link_terms, ("nx", "ny"), split_axis=0, concat_axis=0, tiled=True),
            col_ids,
            width,
        )
        hidden = jnp.maximum(summed + bias[layer_idx][None, :], 0.0).astype(jnp.bfloat16)
    finished = lax.all_to_all(hidden, ("nx", "ny"), split_axis=0, concat_axis=1, tiled=True)
    return finished


def kernel(nx, ny, feat_hbm, weight_hbm, row_hbm, col_hbm, live_hbm, bias_hbm, out, feat, row, col, live, bias, isem, w, fsend, fin, act, tsend, trecv, osend, orecv,
           aux, auxs, colx, rsend, rrecv, psend, precv, colr, wsem, fs, fr, xs, xr, ts, tr, os, orr, rs, rr, ps, pr):
    nd = nx * ny
    layers = bias.shape[0]
    block = w.shape[-1]
    width = bias.shape[1] // block
    rows = feat.shape[0]
    images = rows * nd
    half = images // CHUNKS
    per = nd // CHUNKS
    f32 = jnp.float32
    my_x, my_z = lax.axis_index("nx"), lax.axis_index("ny")
    me = my_x * ny + my_z

    hz = ny // 2
    hi, lo = my_z // hz, my_z % hz
    zs = [(1 - hi) * hz + (lo + i) % hz for i in range(hz)] + [hi * hz + (lo + i) % hz for i in range(1, hz)] + [my_z]
    peers = [((my_x + i) % nx, z, i == 0 and n == ny - 1) for n, z in enumerate(zs) for i in list(range(1, nx)) + [0]]

    def place(a, b):
        return (a % CHUNKS) * per + (a // CHUNKS) * ny + b

    def at(a, b):
        return {"nx": a, "ny": b}

    my_place = place(my_x, my_z)

    loads = [
        pltpu.make_async_copy(src, dst, isem.at[n])
        for n, (src, dst) in enumerate(((feat_hbm, feat), (bias_hbm, bias), (col_hbm, col), (row_hbm, row), (live_hbm, live)))
    ]
    for load in loads:
        load.start()
    for l in range(layers):
        pltpu.make_async_copy(weight_hbm.at[l, 0], w.at[l], wsem.at[l]).start()
    barrier = pltpu.get_barrier_semaphore()
    for a, b, own in peers:
        if not own:
            pl.semaphore_signal(barrier, inc=1, device_id=at(a, b), device_id_type=MESH)

    for load in loads:
        load.wait()
    for j in range(nd):
        for r in range(width):
            s = (j * width + r) * block
            fsend[j, r] = feat[:, s:s + block]
    lane = lax.broadcasted_iota(jnp.int32, (1, block), 1)
    auxs[...] = jnp.zeros_like(auxs)
    for r in range(width):
        auxs[r:r + 1, :] = bias[layers - 1:layers, r * block:(r + 1) * block]
    for l in range(layers):
        cols = jnp.zeros((1, block), jnp.int32)
        for s in range(nd):
            cols = jnp.where(lane == s, col[l, 0, s], cols)
        auxs[width + l:width + l + 1, :] = cols.astype(f32)
    pl.semaphore_wait(barrier, nd - 1)

    pending = []

    def send(src, dst, send_sem, recv_sem, a, b, own):
        if own:
            pltpu.make_async_copy(src, dst, recv_sem).start()
        else:
            c = pltpu.make_async_remote_copy(src, dst, send_sem, recv_sem, device_id=at(a, b), device_id_type=MESH)
            c.start()
            pending.append(c)

    def arrived(ref, sem):
        pltpu.make_async_copy(ref, ref, sem).wait()

    for k, (a, b, own) in enumerate(peers):
        send(fsend.at[a * ny + b], fin.at[my_place], fs.at[k], fr.at[my_place], a, b, own)
    for k, (a, b, own) in enumerate(peers):
        send(auxs, aux.at[me], xs.at[k], xr.at[me], a, b, own)

    def product(l, c, e):
        x = act[row[l, 0, e], c * half:(c + 1) * half, :]
        t = jnp.dot(x, w[l, e], preferred_element_type=f32)
        return (t * live[l, 0, e].astype(f32)).astype(jnp.bfloat16)

    far_z, relay_z = (1 - hi) * hz, hi + hz - 1
    relay = my_z == relay_z
    slot = my_x * hz + lo
    guarded = []

    def source(n):
        return (n // hz) * ny + hi * hz + n % hz

    def send_terms(l, c):
        order = list(range(1, nx)) + [0]
        for k, i in enumerate(order):
            for n in range(hz):
                rsend[l, c, k, n] = product(l, c, (my_x + i) % nx * ny + far_z + n)
        for k, i in enumerate(order):
            a = (my_x + i) % nx
            src, dst = rsend.at[l, c, k], rrecv.at[l, c, slot]
            cp = pltpu.make_async_remote_copy(
                src, dst, rs.at[l, c, k], rr.at[l, c, slot], device_id=at(a, relay_z), device_id_type=MESH
            )
            if i == 0:
                @pl.when(relay)
                def _():
                    pltpu.make_async_copy(src, dst, rr.at[l, c, slot]).start()

                @pl.when(jnp.logical_not(relay))
                def _():
                    cp.start()
                guarded.append((jnp.logical_not(relay), cp))
            else:
                cp.start()
                pending.append(cp)
        steps = [(n, i) for n in list(range(1, hz)) + [0] for i in order]
        for k, (n, i) in enumerate(steps):
            tsend[l, c, k] = product(l, c, (my_x + i) % nx * ny + hi * hz + (lo + n) % hz)
        k = 0
        for n in list(range(1, hz)) + [0]:
            b = hi * hz + (lo + n) % hz
            for i in list(range(1, nx)) + [0]:
                a = (my_x + i) % nx
                send(tsend.at[l, c, k], trecv.at[l, c, slot], ts.at[l, c, k], tr.at[l, c, slot], a, b, n == 0 and i == 0)
                k += 1

    def forward(l, c):
        rows_of = [[(l * hz + i) * nd + source(n) for n in range(nx * hz)] for i in range(hz)]
        cps = [
            pltpu.make_async_remote_copy(
                psend.at[l, c, i], precv.at[l, c], ps.at[l, c, i], pr.at[l, c],
                device_id=at(my_x, far_z + i), device_id_type=MESH
            )
            for i in range(hz)
        ]

        @pl.when(relay)
        def _():
            for n in range(nx * hz):
                arrived(rrecv.at[l, c, n], rr.at[l, c, n])
            for i in range(hz):
                for t0 in range(0, half, 32):
                    acc = [jnp.zeros((32, block), f32) for q in range(width)]
                    for n in range(nx * hz):
                        t = rrecv[l, c, n, i, t0:t0 + 32, :].astype(f32)
                        v = colr[pl.ds(rows_of[i][n], 1)][0]
                        v = jnp.concatenate([v] * 4, axis=0)
                        for q in range(width):
                            acc[q] = acc[q] + jnp.where(v == float(q), t, 0.0)
                    for q in range(width):
                        psend[l, c, i, q, t0:t0 + 32, :] = acc[q].astype(jnp.bfloat16)
                cps[i].start()
        guarded.extend((relay, cp) for cp in cps)

    def send_last(c):
        l = layers - 1
        for e in range(nd):
            t = product(l, c, e).astype(f32).reshape(per, rows, block)
            osend[c * per:(c + 1) * per, e] = t.astype(jnp.bfloat16)
        core, far = my_x % CHUNKS, my_x // CHUNKS
        groups = nx // CHUNKS
        k = 0
        for n, b in enumerate(zs):
            for i in list(range(1, groups)) + [0]:
                a = ((far + i) % groups) * CHUNKS + c
                src, dst = osend.at[place(a, b)], orecv.at[me]
                cp = pltpu.make_async_remote_copy(src, dst, os.at[c, k], orr.at[me], device_id=at(a, b), device_id_type=MESH)
                k += 1
                if i == 0 and n == ny - 1:
                    @pl.when(core == c)
                    def _():
                        pltpu.make_async_copy(src, dst, orr.at[me]).start()

                    @pl.when(core != c)
                    def _():
                        cp.start()
                    lasts.append((c, cp))
                else:
                    cp.start()
                    pending.append(cp)

    lasts = []

    for c in range(CHUNKS):
        for p in range(c * per, (c + 1) * per):
            arrived(fin.at[p], fr.at[p])
        for r in range(width):
            x = fin[c * per:(c + 1) * per, r].astype(f32).reshape(half, block)
            act[r, c * half:(c + 1) * half, :] = x.astype(jnp.bfloat16)
        if c == 0:
            arrived(w.at[0], wsem.at[0])
        send_terms(0, c)

    for g in range(nd):
        arrived(aux.at[g], xr.at[g])
    eye = lax.broadcasted_iota(jnp.int32, (nd, block), 0) == lax.broadcasted_iota(jnp.int32, (nd, block), 1)
    ones = jnp.ones((block, block), jnp.bfloat16)
    for e in range(nd):
        last = width + layers - 1
        v = jnp.where(eye, aux[e, last:last + 1, :], 0.0).astype(jnp.bfloat16)
        colx[e * nd:(e + 1) * nd, :] = jnp.dot(v, ones, preferred_element_type=f32)

    for l in range(layers - 1):
        for i in range(hz):
            v = jnp.where(eye, aux[my_x * ny + far_z + i, width + l:width + l + 1, :], 0.0).astype(jnp.bfloat16)
            m = jnp.dot(v, ones, preferred_element_type=f32)
            k = (l * hz + i) * nd
            colr[k:k + nd] = jnp.broadcast_to(m[:, None, :], (nd, 8, block))
    for c in range(CHUNKS):
        forward(0, c)

    tile = 32
    for l in range(1, layers):
        arrived(w.at[l], wsem.at[l])
        for c in range(CHUNKS):
            for n in range(nx * hz):
                arrived(trecv.at[l - 1, c, n], tr.at[l - 1, c, n])
            arrived(precv.at[l - 1, c], pr.at[l - 1, c])
            for t0 in range(0, half, tile):
                acc = [jnp.broadcast_to(bias[l - 1:l, q * block:(q + 1) * block], (tile, block)) for q in range(width)]
                acc = [acc[q] + precv[l - 1, c, q, t0:t0 + tile, :].astype(f32) for q in range(width)]
                for n in range(nx * hz):
                    t = trecv[l - 1, c, n, t0:t0 + tile, :].astype(f32)
                    where = col[l - 1, 0, source(n)]
                    for q in range(width):
                        acc[q] = acc[q] + t * (where == q).astype(f32)
                for q in range(width):
                    act[q, c * half + t0:c * half + t0 + tile, :] = jnp.maximum(acc[q], 0.0).astype(jnp.bfloat16)
            if l < layers - 1:
                send_terms(l, c)
            else:
                send_last(c)
        if l < layers - 1:
            for c in range(CHUNKS):
                forward(l, c)

    for g in range(nd):
        arrived(orecv.at[g], orr.at[g])
    for e in range(nd):
        acc = [jnp.broadcast_to(aux[e, q:q + 1, :], (rows, block)) for q in range(width)]
        for g in range(nd):
            t = orecv[g, e].astype(f32)
            where = jnp.broadcast_to(colx[e * nd + g:e * nd + g + 1, :], (rows, block))
            for q in range(width):
                acc[q] = acc[q] + jnp.where(where == float(q), t, 0.0)
        for q in range(width):
            s = (e * width + q) * block
            out[:, s:s + block] = jnp.maximum(acc[q], 0.0).astype(jnp.bfloat16)

    for cp in pending:
        cp.wait_send()
    for started, cp in guarded:
        @pl.when(started)
        def _():
            cp.wait_send()
    for c, cp in lasts:
        @pl.when(my_x % CHUNKS != c)
        def _():
            cp.wait_send()


def fused(nx, ny, features, link_weight, link_row, link_col, link_live, bias):
    nd = nx * ny
    layers = bias.shape[0]
    block = link_weight.shape[-1]
    width = bias.shape[1] // block
    rows = features.shape[0]
    half = rows * nd // CHUNKS
    hz = ny // 2
    bf16 = jnp.bfloat16
    vmem = pl.BlockSpec(memory_space=pltpu.VMEM)
    counts = pltpu.SMEM((layers, 1, nd), jnp.int32)
    dma = pltpu.SemaphoreType.DMA
    return pl.pallas_call(
        functools.partial(kernel, nx, ny),
        out_shape=jax.ShapeDtypeStruct(features.shape, bf16),
        in_specs=[pl.BlockSpec(memory_space=pl.ANY)] * 6,
        out_specs=vmem,
        scratch_shapes=[
            pltpu.VMEM(features.shape, bf16),
            counts, counts, counts,
            pltpu.VMEM(bias.shape, jnp.float32),
            dma((5,)),
            pltpu.VMEM((layers, nd, block, block), bf16),
            pltpu.VMEM((nd, width, rows, block), bf16),
            pltpu.VMEM((nd, width, rows, block), bf16),
            pltpu.VMEM((width, rows * nd, block), bf16),
            pltpu.VMEM((layers - 1, CHUNKS, nx * hz, half, block), bf16),
            pltpu.VMEM((layers - 1, CHUNKS, nx * hz, half, block), bf16),
            pltpu.VMEM((nd, nd, rows, block), bf16),
            pltpu.VMEM((nd, nd, rows, block), bf16),
            pltpu.VMEM((nd, 8, block), jnp.float32),
            pltpu.VMEM((8, block), jnp.float32),
            pltpu.VMEM((nd * nd, block), jnp.float32),
            pltpu.VMEM((layers - 1, CHUNKS, nx, hz, half, block), bf16),
            pltpu.VMEM((layers - 1, CHUNKS, nx * hz, hz, half, block), bf16),
            pltpu.VMEM((layers - 1, CHUNKS, hz, width, half, block), bf16),
            pltpu.VMEM((layers - 1, CHUNKS, width, half, block), bf16),
            pltpu.VMEM(((layers - 1) * hz * nd, 8, block), jnp.float32),
            dma((layers,)),
            dma((nd,)), dma((nd,)), dma((nd,)), dma((nd,)),
            dma((layers - 1, CHUNKS, nx * hz)), dma((layers - 1, CHUNKS, nx * hz)),
            dma((CHUNKS, nd)), dma((nd,)),
            dma((layers - 1, CHUNKS, nx)), dma((layers - 1, CHUNKS, nx * hz)),
            dma((layers - 1, CHUNKS, hz)), dma((layers - 1, CHUNKS)),
        ],
        compiler_params=pltpu.CompilerParams(
            collective_id=0, has_side_effects=True, vmem_limit_bytes=60 * 1024 * 1024
        ),
    )(features, link_weight, link_row, jnp.transpose(link_col, (0, 2, 1)), link_live, bias)


def solution(mesh):
    placed = (
        P(("nx", "ny", "img"), None),
        P(None, ("nx", "ny"), None, None, None),
        P(None, ("nx", "ny"), None),
        P(None, None, ("nx", "ny")),
        P(None, ("nx", "ny"), None),
        P(None, ("nx", "ny")),
    )
    nx, ny = mesh.shape["nx"], mesh.shape["ny"]

    def run(features, link_weight, link_row, link_col, link_live, bias):
        block = link_weight.shape[-1]
        rows = features.shape[0]
        width = bias.shape[1] // block
        fits = (
            rows % 8 == 0 and nx % CHUNKS == 0 and ny % 2 == 0 and block == 128
            and nx * ny <= 32 and width + bias.shape[0] <= 8 and (rows * nx * ny) % (32 * CHUNKS) == 0 and bias.shape[0] > 1
        )
        step = functools.partial(fused, nx, ny) if fits else local
        return step(features, link_weight, link_row, link_col, link_live, bias)

    return jax.shard_map(
        run, mesh=mesh, in_specs=placed, out_specs=P(("nx", "ny", "img"), None), check_vma=False
    )
```

profile of v0, /device:TPU:1, one launch (start us, length us, event | category | flops | bytes accessed | tf_op | source)
XLA Modules:
  0.0 51.3 jit_solution(12575116256978230795)
XLA Ops:
  0.0 49.7 %shard_map.64 = bf16[8,8192]{1,0:T(8,128)(2,1)} custom-call(bf16[8,8192]{1,0:T(8,128)(2,1)} %feat_hbm.1, bf16[3,1,16,128,128]{4,3,2,1,0:T(8,128)(2,1)} %weight_hbm.1, s32[3,1,16]{2,1,0:T(1,128)} %row_hbm.1, s32[3,1,16]{2,1,0:T(1,128)} %bitcast.1, s32[3,1,16]{2,1,0:T(1,128)} %live_hbm.1, f32[3,512]{1,0:T(4,128)} %bias_hbm.1), custom_call_target="tpu_custom_call" | custom-call | tf_op jit(solution)/shard_map/pallas_call | solution.py:319
  49.8 1.6 %copy.8 = bf16[8,8192]{1,0:T(8,128)(2,1)} copy(bf16[8,8192]{1,0:T(8,128)(2,1)} %shard_map.64) | data formatting | bytes 262144
where the time goes:
time: 51.5 us; the launch traced here: 51.3 us
  Pallas kernels  49.7 us (97%)
  local copies, waits for them, and re-layouts  1.57 us (3%)
    pallas_call x1, Pallas kernels, fused(): pl.pallas_call(functools.partial(kernel, nx, ny), out_shape=jax.ShapeDtyp...  49.7 us
    unnamed x1, local copies, waits for them, and re-layouts  1.57 us

commit v1 on v0

--- a/solution.py
+++ b/solution.py
@@ -318,7 +318,7 @@
     dma = pltpu.SemaphoreType.DMA
     return pl.pallas_call(
         functools.partial(kernel, nx, ny),
-        out_shape=jax.ShapeDtypeStruct(features.shape, bf16),
+        out_shape=pltpu.VMEM(features.shape, bf16),
         in_specs=[pl.BlockSpec(memory_space=pl.ANY)] * 6,
         out_specs=vmem,
         scratch_shapes=[

time: 51.5 us -> 49.9 us (0.969)
  local copies, waits for them, and re-layouts: 1.57 us -> 0.66 us
  Pallas kernels: 49.7 us -> 49.1 us
    unnamed x1, local copies, waits for them, and re-layouts: 1.57 us -> 0.66 us
    pallas_call x1, Pallas kernels: 49.7 us -> 49.1 us  [fused(): pl.pallas_call(functools.partial(kernel, nx, ny), out_shape=pltpu.VMEM(fe...]
where the time goes in v1:
time: 49.9 us; the launch traced here: 49.8 us
  Pallas kernels  49.1 us (98%)
  local copies, waits for them, and re-layouts  0.66 us (1%)
    pallas_call x1, Pallas kernels, fused(): pl.pallas_call(functools.partial(kernel, nx, ny), out_shape=pltpu.VMEM(fe...  49.1 us

profile of v1, /device:TPU:1, one launch (start us, length us, event | category | flops | bytes accessed | tf_op | source)
XLA Modules:
  0.0 49.8 jit_solution(6568714482812972524)
XLA Ops:
  0.0 49.1 %shard_map.64 = bf16[8,8192]{1,0:T(8,128)(2,1)S(1)} custom-call(bf16[8,8192]{1,0:T(8,128)(2,1)} %feat_hbm.1, bf16[3,1,16,128,128]{4,3,2,1,0:T(8,128)(2,1)} %weight_hbm.1, s32[3,1,16]{2,1,0:T(1,128)} %row_hbm.1, s32[3,1,16]{2,1,0:T(1,128)} %bitcast.1, s32[3,1,16]{2,1,0:T(1,128)} %live_hbm.1, f32[3,512]{1,0:T(4,128)} %bias_hbm.1), custom_call_target="tpu_custom_call" | custom-call | tf_op jit(solution)/shard_map/pallas_call | solution.py:319
  49.1 0.7 %copy.8 = bf16[8,8192]{1,0:T(8,128)(2,1)} copy(bf16[8,8192]{1,0:T(8,128)(2,1)S(1)} %shard_map.64) | data formatting | bytes 262144

commit v2 on v1

v2 whole, which is shorter than its diff:
```python
import functools

import jax
import jax.numpy as jnp
from jax import lax
from jax.experimental import pallas as pl
from jax.experimental.pallas import tpu as pltpu
from jax.sharding import PartitionSpec as P

MESH = pl.DeviceIdType.MESH
LAG = 2


def combine_links(received, col_ids, width):
    onehot = (col_ids[:, None] == jnp.arange(width, dtype=jnp.int32)[None, :]).astype(jnp.bfloat16)
    summed = jnp.einsum("dq,dis->iqs", onehot, received, preferred_element_type=jnp.float32)
    return summed.reshape(summed.shape[0], width * received.shape[2])


def link_products(blocks, weights, row_ids, live_mask):
    masked = weights * live_mask.astype(jnp.bfloat16)[:, None, None]
    gathered = jnp.take(blocks, row_ids, axis=1)
    result = jnp.einsum(
        "ier,ers->eis", gathered, masked, preferred_element_type=jnp.float32
    ).astype(jnp.bfloat16)
    return result


def local(features, link_weight, link_row, link_col, link_live, bias):
    block_size = link_weight.shape[-1]
    width = bias.shape[1] // block_size
    hidden = lax.all_to_all(features, ("nx", "ny"), split_axis=1, concat_axis=0, tiled=True)
    image_rows = hidden.shape[0]
    for layer_idx in range(bias.shape[0]):
        blocks = hidden.reshape(image_rows, width, block_size)
        link_terms = link_products(
            blocks, link_weight[layer_idx, 0], link_row[layer_idx, 0], link_live[layer_idx, 0]
        )
        col_ids = link_col[layer_idx, :, 0]
        summed = combine_links(
            lax.all_to_all(link_terms, ("nx", "ny"), split_axis=0, concat_axis=0, tiled=True),
            col_ids,
            width,
        )
        hidden = jnp.maximum(summed + bias[layer_idx][None, :], 0.0).astype(jnp.bfloat16)
    finished = lax.all_to_all(hidden, ("nx", "ny"), split_axis=0, concat_axis=1, tiled=True)
    return finished


def kernel(nx, ny, feat_hbm, weight_hbm, row_hbm, col_hbm, live_hbm, bias_hbm, out, feat, row, col, live, bias, isem, w, wsem,
           fin, fs, fr, act, auxs, aux, xs, xr, colx, colr, tsend, trecv, ts, tr, rsend, rrecv, rs, ro, rr, psend, precv, ps, pr,
           lsend, orecv, ls, orr, qrecv, qr, usend, urecv, us, ur, pre):
    nd = nx * ny
    layers = bias.shape[0]
    block = w.shape[-1]
    width = bias.shape[1] // block
    rows = feat.shape[0]
    hz = ny // 2
    chunks = 2 * hz
    per = nd // chunks
    size = per * rows
    near = nx * hz
    f32, bf16 = jnp.float32, jnp.bfloat16
    my_x, my_z = lax.axis_index("nx"), lax.axis_index("ny")
    me = my_x * ny + my_z
    hi, lo = my_z // hz, my_z % hz
    far_z, relay_z = (1 - hi) * hz, hi + hz - 1
    relay = my_z == relay_z
    slot = my_x * hz + lo

    zs = [(1 - hi) * hz + (lo + i) % hz for i in range(hz)] + [hi * hz + (lo + i) % hz for i in range(1, hz)] + [my_z]
    peers = [((my_x + i) % nx, z, i == 0 and n == ny - 1) for n, z in enumerate(zs) for i in list(range(1, nx)) + [0]]

    def place(a, b):
        return ((a % 2) * hz + b % hz) * per + (a // 2) * 2 + b // hz

    def remote(src, dst, send_sem, recv_sem, a, b):
        return pltpu.make_async_remote_copy(src, dst, send_sem, recv_sem, device_id={"nx": a, "ny": b}, device_id_type=MESH)

    def send(src, dst, send_sem, recv_sem, a, b, own):
        if own:
            pltpu.make_async_copy(src, dst, recv_sem).start()
        else:
            remote(src, dst, send_sem, recv_sem, a, b).start()

    def arrived(ref, sem):
        pltpu.make_async_copy(ref, ref, sem).wait()

    loads = [
        pltpu.make_async_copy(src, dst, isem.at[n])
        for n, (src, dst) in enumerate(((feat_hbm, feat), (bias_hbm, bias), (col_hbm, col), (row_hbm, row), (live_hbm, live)))
    ]
    for load in loads:
        load.start()
    for l in range(layers):
        pltpu.make_async_copy(weight_hbm.at[l, 0], w.at[l], wsem.at[l]).start()
    barrier = pltpu.get_barrier_semaphore()
    for a, b, own in peers:
        if not own:
            pl.semaphore_signal(barrier, inc=1, device_id={"nx": a, "ny": b}, device_id_type=MESH)

    for load in loads:
        load.wait()
    lane = lax.broadcasted_iota(jnp.int32, (1, block), 1)
    auxs[...] = jnp.zeros_like(auxs)
    for r in range(width):
        auxs[r:r + 1, :] = bias[layers - 1:layers, r * block:(r + 1) * block]
    for l in range(layers):
        cols = jnp.zeros((1, block), jnp.int32)
        for s in range(nd):
            cols = jnp.where(lane == s, col[l, 0, s], cols)
        auxs[width + l:width + l + 1, :] = cols.astype(f32)
    pl.semaphore_wait(barrier, nd - 1)

    my_place = place(my_x, my_z)
    my_chunk = my_place // per
    span = width * block
    for a, b, own in peers:
        at = pl.multiple_of((a * ny + b) * span, span)
        send(feat.at[:, pl.ds(at, span)], fin.at[my_place], fs, fr.at[my_chunk], a, b, own)
    for a, b, own in peers:
        send(auxs, aux.at[me], xs, xr, a, b, own)

    def product(l, c, e):
        x = act[row[l, 0, e], c * size:(c + 1) * size, :]
        t = jnp.dot(x, w[l, e], preferred_element_type=f32)
        return t * live[l, 0, e].astype(f32)

    def source(n):
        return (n // hz) * ny + hi * hz + n % hz

    order = list(range(1, nx)) + [0]
    steps = [(n, i) for n in list(range(1, hz)) + [0] for i in order]

    def send_terms(l, c):
        k = l * chunks + c
        for j, i in enumerate(order):
            for n in range(hz):
                rsend[j, k, n] = product(l, c, (my_x + i) % nx * ny + far_z + n).astype(bf16)
        for j, i in enumerate(order):
            a = (my_x + i) % nx
            src, dst = rsend.at[j, k], rrecv.at[k, slot]
            if i == 0:
                @pl.when(relay)
                def _():
                    pltpu.make_async_copy(src, dst, rr.at[k]).start()

                @pl.when(jnp.logical_not(relay))
                def _():
                    remote(src, dst, ro, rr.at[k], a, relay_z).start()
            else:
                remote(src, dst, rs, rr.at[k], a, relay_z).start()
        for j, (n, i) in enumerate(steps):
            tsend[j, k] = product(l, c, (my_x + i) % nx * ny + hi * hz + (lo + n) % hz).astype(bf16)
        for j, (n, i) in enumerate(steps):
            a, b = (my_x + i) % nx, hi * hz + (lo + n) % hz
            send(tsend.at[j, k], trecv.at[k, slot], ts, tr.at[k], a, b, n == 0 and i == 0)

    def forward(l, c):
        k = l * chunks + c

        @pl.when(relay)
        def _():
            arrived(rrecv.at[k], rr.at[k])
            for i in range(hz):
                acc = [jnp.zeros((size, block), f32) for q in range(width)]
                for n in range(near):
                    t = rrecv[k, n, i].astype(f32)
                    v = colr[pl.ds((l * hz + i) * nd + source(n), 1)][0]
                    v = jnp.concatenate([v] * (size // 8), axis=0)
                    for q in range(width):
                        acc[q] = acc[q] + jnp.where(v == float(q), t, 0.0)
                for q in range(width):
                    psend[k, i, q] = acc[q].astype(bf16)
                remote(psend.at[k, i], precv.at[k], ps, pr.at[k], my_x, far_z + i).start()

    def collect(l, c):
        k = l * chunks + c
        arrived(trecv.at[k], tr.at[k])
        arrived(precv.at[k], pr.at[k])
        acc = [jnp.broadcast_to(bias[l:l + 1, q * block:(q + 1) * block], (size, block)) for q in range(width)]
        acc = [acc[q] + precv[k, q].astype(f32) for q in range(width)]
        for n in range(near):
            t = trecv[k, n].astype(f32)
            where = col[l, 0, source(n)]
            for q in range(width):
                acc[q] = acc[q] + t * (where == q).astype(f32)
        for q in range(width):
            act[q, c * size:(c + 1) * size, :] = jnp.maximum(acc[q], 0.0).astype(bf16)

    def owners(c):
        p, q = c // hz, c % hz
        return [(2 * j + p, (1 - hi) * hz + q, 2 * j + 1 - hi) for j in range(nx // 2)], [
            (2 * j + p, hi * hz + q, 2 * j + hi) for j in range(nx // 2)]

    def send_last(c):
        l = layers - 1
        p, q = c // hz, c % hz
        far, close = owners(c)
        for e in range(nd):
            t = product(l, c, e).reshape(per, rows, block)
            lsend[c * per:(c + 1) * per, e] = t.astype(bf16)
        for a, b, o in far:
            src, dst = lsend.at[c * per + o], qrecv.at[q, slot]
            mine = jnp.logical_and(relay, my_x == a)

            @pl.when(mine)
            def _():
                pltpu.make_async_copy(src, dst, qr.at[q]).start()

            @pl.when(jnp.logical_not(mine))
            def _():
                remote(src, dst, ls, qr.at[q], a, relay_z).start()
        for a, b, o in close:
            src, dst = lsend.at[c * per + o], orecv.at[slot]
            mine = jnp.logical_and(my_z == b, my_x == a)

            @pl.when(mine)
            def _():
                pltpu.make_async_copy(src, dst, orr).start()

            @pl.when(jnp.logical_not(mine))
            def _():
                remote(src, dst, ls, orr, a, b).start()

    def forward_last(c):
        p, q = c // hz, c % hz

        @pl.when(jnp.logical_and(relay, my_x % 2 == p))
        def _():
            arrived(qrecv.at[q], qr.at[q])
            for e in range(nd):
                acc = [jnp.zeros((rows, block), f32) for r in range(width)]
                for n in range(near):
                    t = qrecv[q, n, e].astype(f32)
                    v = jnp.broadcast_to(colx[pl.ds(e * nd + source(n), 1), :], (rows, block))
                    for r in range(width):
                        acc[r] = acc[r] + jnp.where(v == float(r), t, 0.0)
                for r in range(width):
                    usend[q, e, r] = acc[r].astype(bf16)
            remote(usend.at[q], urecv, us, ur, my_x, far_z + q).start()

    for c in range(chunks):
        arrived(fin.at[c * per:(c + 1) * per], fr.at[c])
        for r in range(width):
            x = fin[c * per:(c + 1) * per, :, r * block:(r + 1) * block].astype(f32).reshape(size, block)
            act[r, c * size:(c + 1) * size, :] = x.astype(bf16)
        if c == 0:
            arrived(w.at[0], wsem.at[0])
        send_terms(0, c)

    arrived(aux, xr)
    eye = lax.broadcasted_iota(jnp.int32, (nd, block), 0) == lax.broadcasted_iota(jnp.int32, (nd, block), 1)
    ones = jnp.ones((block, block), bf16)
    for l in range(layers - 1):
        for i in range(hz):
            v = jnp.where(eye, aux[my_x * ny + far_z + i, width + l:width + l + 1, :], 0.0).astype(bf16)
            m = jnp.dot(v, ones, preferred_element_type=f32)
            k = (l * hz + i) * nd
            colr[k:k + nd] = jnp.broadcast_to(m[:, None, :], (nd, 8, block))
    for e in range(nd):
        last = width + layers - 1
        v = jnp.where(eye, aux[e, last:last + 1, :], 0.0).astype(bf16)
        colx[e * nd:(e + 1) * nd, :] = jnp.dot(v, ones, preferred_element_type=f32)

    total = layers * chunks

    def relay_step(k):
        if k < total - chunks:
            forward(k // chunks, k % chunks)
        elif k < total:
            forward_last(k % chunks)

    for k in range(LAG):
        relay_step(k)
    for k in range(total - chunks):
        relay_step(k + LAG)
        l, c = k // chunks, k % chunks
        collect(l, c)
        if c == 0:
            arrived(w.at[l + 1], wsem.at[l + 1])
        if l + 1 < layers - 1:
            send_terms(l + 1, c)
        else:
            send_last(c)
    for k in range(total - chunks + LAG, total):
        relay_step(k)

    arrived(orecv, orr)
    for e in range(nd):
        acc = [jnp.broadcast_to(aux[e, q:q + 1, :], (rows, block)) for q in range(width)]
        for n in range(near):
            t = orecv[n, e].astype(f32)
            v = jnp.broadcast_to(colx[pl.ds(e * nd + source(n), 1), :], (rows, block))
            for q in range(width):
                acc[q] = acc[q] + jnp.where(v == float(q), t, 0.0)
        for q in range(width):
            pre[e * width + q] = acc[q]
    arrived(urecv, ur)
    for e in range(nd):
        for q in range(width):
            s = (e * width + q) * block
            out[:, s:s + block] = jnp.maximum(pre[e * width + q] + urecv[e, q].astype(f32), 0.0).astype(bf16)

    arrived(fin.at[0:nd - 1], fs)
    arrived(aux.at[0:nd - 1], xs)
    arrived(tsend.at[0:near - 1], ts)
    arrived(rsend.at[0:nx - 1], rs)

    @pl.when(relay)
    def _():
        arrived(psend, ps)
        arrived(usend, us)
        arrived(lsend.at[0:nd - 1 - hz], ls)

    @pl.when(jnp.logical_not(relay))
    def _():
        arrived(rsend.at[nx - 1], ro)
        arrived(lsend.at[0:nd - 1], ls)


def fused(nx, ny, features, link_weight, link_row, link_col, link_live, bias):
    nd = nx * ny
    layers = bias.shape[0]
    block = link_weight.shape[-1]
    width = bias.shape[1] // block
    rows = features.shape[0]
    hz = ny // 2
    chunks = 2 * hz
    per = nd // chunks
    size = per * rows
    near = nx * hz
    steps = (layers - 1) * chunks
    bf16, f32 = jnp.bfloat16, jnp.float32
    vmem = pltpu.VMEM
    counts = pltpu.SMEM((layers, 1, nd), jnp.int32)
    dma = pltpu.SemaphoreType.DMA
    return pl.pallas_call(
        functools.partial(kernel, nx, ny),
        out_shape=vmem(features.shape, bf16),
        in_specs=[pl.BlockSpec(memory_space=pl.ANY)] * 6,
        out_specs=pl.BlockSpec(memory_space=vmem),
        scratch_shapes=[
            vmem(features.shape, bf16), counts, counts, counts, vmem(bias.shape, f32), dma((5,)),
            vmem((layers, nd, block, block), bf16), dma((layers,)),
            vmem((nd, rows, width * block), bf16), dma, dma((chunks,)),
            vmem((width, rows * nd, block), bf16),
            vmem((8, block), f32), vmem((nd, 8, block), f32), dma, dma,
            vmem((nd * nd, block), f32), vmem(((layers - 1) * hz * nd, 8, block), f32),
            vmem((near, steps, size, block), bf16), vmem((steps, near, size, block), bf16), dma, dma((steps,)),
            vmem((nx, steps, hz, size, block), bf16), vmem((steps, near, hz, size, block), bf16), dma, dma, dma((steps,)),
            vmem((steps, hz, width, size, block), bf16), vmem((steps, width, size, block), bf16), dma, dma((steps,)),
            vmem((nd, nd, rows, block), bf16), vmem((near, nd, rows, block), bf16), dma, dma,
            vmem((hz, near, nd, rows, block), bf16), dma((hz,)),
            vmem((hz, nd, width, rows, block), bf16), vmem((nd, width, rows, block), bf16), dma, dma,
            vmem((nd * width, rows, block), f32),
        ],
        compiler_params=pltpu.CompilerParams(
            collective_id=0, has_side_effects=True, vmem_limit_bytes=60 * 1024 * 1024
        ),
    )(features, link_weight, link_row, jnp.transpose(link_col, (0, 2, 1)), link_live, bias)


def solution(mesh):
    placed = (
        P(("nx", "ny", "img"), None),
        P(None, ("nx", "ny"), None, None, None),
        P(None, ("nx", "ny"), None),
        P(None, None, ("nx", "ny")),
        P(None, ("nx", "ny"), None),
        P(None, ("nx", "ny")),
    )
    nx, ny = mesh.shape["nx"], mesh.shape["ny"]

    def run(features, link_weight, link_row, link_col, link_live, bias):
        block = link_weight.shape[-1]
        rows = features.shape[0]
        width = bias.shape[1] // block
        fits = (
            rows % 8 == 0 and nx % 2 == 0 and ny % 2 == 0 and block == 128
            and nx * ny <= 32 and width + bias.shape[0] <= 8 and (nx * rows) % 16 == 0 and bias.shape[0] > 1
        )
        step = functools.partial(fused, nx, ny) if fits else local
        return step(features, link_weight, link_row, link_col, link_live, bias)

    return jax.shard_map(
        run, mesh=mesh, in_specs=placed, out_specs=P(("nx", "ny", "img"), None), check_vma=False
    )
```

time: 49.9 us -> 41.6 us (0.83)
  Pallas kernels: 49.1 us -> 40.8 us
    pallas_call x1, Pallas kernels: 49.1 us -> 40.8 us  [fused(): pl.pallas_call(functools.partial(kernel, nx, ny), out_shape=vmem(features...]
where the time goes in v2:
time: 41.6 us; the launch traced here: 41.5 us
  Pallas kernels  40.8 us (98%)
  local copies, waits for them, and re-layouts  0.66 us (2%)
    pallas_call x1, Pallas kernels, fused(): pl.pallas_call(functools.partial(kernel, nx, ny), out_shape=vmem(features...  40.8 us

profile of v2, /device:TPU:1, one launch (start us, length us, event | category | flops | bytes accessed | tf_op | source)
XLA Modules:
  0.0 41.5 jit_solution(1452822302763906757)
XLA Ops:
  0.0 40.8 %shard_map.64 = bf16[8,8192]{1,0:T(8,128)(2,1)S(1)} custom-call(bf16[8,8192]{1,0:T(8,128)(2,1)} %feat_hbm.1, bf16[3,1,16,128,128]{4,3,2,1,0:T(8,128)(2,1)} %weight_hbm.1, s32[3,1,16]{2,1,0:T(1,128)} %row_hbm.1, s32[3,1,16]{2,1,0:T(1,128)} %bitcast.1, s32[3,1,16]{2,1,0:T(1,128)} %live_hbm.1, f32[3,512]{1,0:T(4,128)} %bias_hbm.1), custom_call_target="tpu_custom_call" | custom-call | tf_op jit(solution)/shard_map/pallas_call | solution.py:338
  40.8 0.7 %copy.8 = bf16[8,8192]{1,0:T(8,128)(2,1)} copy(bf16[8,8192]{1,0:T(8,128)(2,1)S(1)} %shard_map.64) | data formatting | bytes 262144

commit v3 on v2

--- a/solution.py
+++ b/solution.py
@@ -9,6 +9,9 @@
 
 MESH = pl.DeviceIdType.MESH
 LAG = 2
+GROUPS = 4
+DEPTH = 1
+DEPTH_LAST = 1
 
 
 def combine_links(received, col_ids, width):
@@ -61,6 +64,7 @@
     size = per * rows
     near = nx * hz
     f32, bf16 = jnp.float32, jnp.bfloat16
+    part = nd // GROUPS
     my_x, my_z = lax.axis_index("nx"), lax.axis_index("ny")
     me = my_x * ny + my_z
     hi, lo = my_z // hz, my_z % hz
@@ -68,11 +72,13 @@
     relay = my_z == relay_z
     slot = my_x * hz + lo
 
-    zs = [(1 - hi) * hz + (lo + i) % hz for i in range(hz)] + [hi * hz + (lo + i) % hz for i in range(1, hz)] + [my_z]
+    zs = [hi * i + (1 - hi) * (ny - 1 - i) for i in range(hz)] + [hi * hz + (lo + i) % hz for i in range(1, hz)] + [my_z]
     peers = [((my_x + i) % nx, z, i == 0 and n == ny - 1) for n, z in enumerate(zs) for i in list(range(1, nx)) + [0]]
 
     def place(a, b):
-        return ((a % 2) * hz + b % hz) * per + (a // 2) * 2 + b // hz
+        d = (b // hz) * (b - hz) + (1 - b // hz) * (hz - 1 - b)
+        p = a % 2
+        return (p * hz + (1 - p) * d + p * (hz - 1 - d)) * per + (a // 2) * 2 + b // hz
 
     def remote(src, dst, send_sem, recv_sem, a, b):
         return pltpu.make_async_remote_copy(src, dst, send_sem, recv_sem, device_id={"nx": a, "ny": b}, device_id_type=MESH)
@@ -132,29 +138,43 @@
     order = list(range(1, nx)) + [0]
     steps = [(n, i) for n in list(range(1, hz)) + [0] for i in order]
 
+    held = []
+
+    def release(depth):
+        while len(held) > depth:
+            for start in held.pop(0):
+                start()
+
+    def send_bundle(l, c, j, i):
+        k = l * chunks + c
+        a = (my_x + i) % nx
+        src, dst = rsend.at[j, k], rrecv.at[k, slot]
+        if i == 0:
+            @pl.when(relay)
+            def _():
+                pltpu.make_async_copy(src, dst, rr.at[k]).start()
+
+            @pl.when(jnp.logical_not(relay))
+            def _():
+                remote(src, dst, ro, rr.at[k], a, relay_z).start()
+        else:
+            remote(src, dst, rs, rr.at[k], a, relay_z).start()
+
+    def send_near(k, j, n, i):
+        a, b = (my_x + i) % nx, hi * hz + (lo + n) % hz
+        send(tsend.at[j, k], trecv.at[k, slot], ts, tr.at[k], a, b, n == 0 and i == 0)
+
     def send_terms(l, c):
         k = l * chunks + c
         for j, i in enumerate(order):
             for n in range(hz):
                 rsend[j, k, n] = product(l, c, (my_x + i) % nx * ny + far_z + n).astype(bf16)
         for j, i in enumerate(order):
-            a = (my_x + i) % nx
-            src, dst = rsend.at[j, k], rrecv.at[k, slot]
-            if i == 0:
-                @pl.when(relay)
-                def _():
-                    pltpu.make_async_copy(src, dst, rr.at[k]).start()
-
-                @pl.when(jnp.logical_not(relay))
-                def _():
-                    remote(src, dst, ro, rr.at[k], a, relay_z).start()
-            else:
-                remote(src, dst, rs, rr.at[k], a, relay_z).start()
+            send_bundle(l, c, j, i)
+        release(DEPTH - 1)
         for j, (n, i) in enumerate(steps):
             tsend[j, k] = product(l, c, (my_x + i) % nx * ny + hi * hz + (lo + n) % hz).astype(bf16)
-        for j, (n, i) in enumerate(steps):
-            a, b = (my_x + i) % nx, hi * hz + (lo + n) % hz
-            send(tsend.at[j, k], trecv.at[k, slot], ts, tr.at[k], a, b, n == 0 and i == 0)
+        held.append([functools.partial(send_near, k, j, n, i) for j, (n, i) in enumerate(steps)])
 
     def forward(l, c):
         k = l * chunks + c
@@ -188,57 +208,71 @@
         for q in range(width):
             act[q, c * size:(c + 1) * size, :] = jnp.maximum(acc[q], 0.0).astype(bf16)
 
+    def split(c):
+        p = c // hz
+        return p, (1 - p) * (c % hz) + p * (hz - 1 - c % hz)
+
     def owners(c):
-        p, q = c // hz, c % hz
-        return [(2 * j + p, (1 - hi) * hz + q, 2 * j + 1 - hi) for j in range(nx // 2)], [
-            (2 * j + p, hi * hz + q, 2 * j + hi) for j in range(nx // 2)]
+        p, d = split(c)
+        far = (1 - hi) * (hz + d) + hi * (hz - 1 - d)
+        close = hi * (hz + d) + (1 - hi) * (hz - 1 - d)
+        return [(2 * j + p, far, 2 * j + 1 - hi) for j in range(nx // 2)], [(2 * j + p, close, 2 * j + hi) for j in range(nx // 2)]
 
     def send_last(c):
         l = layers - 1
-        p, q = c // hz, c % hz
+        p, q = split(c)
         far, close = owners(c)
         for e in range(nd):
             t = product(l, c, e).reshape(per, rows, block)
             lsend[c * per:(c + 1) * per, e] = t.astype(bf16)
-        for a, b, o in far:
-            src, dst = lsend.at[c * per + o], qrecv.at[q, slot]
-            mine = jnp.logical_and(relay, my_x == a)
-
-            @pl.when(mine)
-            def _():
-                pltpu.make_async_copy(src, dst, qr.at[q]).start()
-
-            @pl.when(jnp.logical_not(mine))
-            def _():
-                remote(src, dst, ls, qr.at[q], a, relay_z).start()
-        for a, b, o in close:
-            src, dst = lsend.at[c * per + o], orecv.at[slot]
-            mine = jnp.logical_and(my_z == b, my_x == a)
-
-            @pl.when(mine)
-            def _():
-                pltpu.make_async_copy(src, dst, orr).start()
-
-            @pl.when(jnp.logical_not(mine))
-            def _():
-                remote(src, dst, ls, orr, a, b).start()
+        for g in range(GROUPS):
+            for a, b, o in far:
+                send_far(c, g, q, a, o)
+        release(DEPTH_LAST - 1)
+        held.append([functools.partial(send_close, c, a, b, o) for a, b, o in close])
+
+    def send_far(c, g, q, a, o):
+        src, dst = lsend.at[c * per + o, g * part:(g + 1) * part], qrecv.at[q, g, slot]
+        mine = jnp.logical_and(relay, my_x == a)
+
+        @pl.when(mine)
+        def _():
+            pltpu.make_async_copy(src, dst, qr.at[q, g]).start()
+
+        @pl.when(jnp.logical_not(mine))
+        def _():
+            remote(src, dst, ls, qr.at[q, g], a, relay_z).start()
+
+    def send_close(c, a, b, o):
+        src, dst = lsend.at[c * per + o], orecv.at[slot]
+        mine = jnp.logical_and(my_z == b, my_x == a)
+
+        @pl.when(mine)
+        def _():
+            pltpu.make_async_copy(src, dst, orr).start()
+
+        @pl.when(jnp.logical_not(mine))
+        def _():
+            remote(src, dst, ls, orr, a, b).start()
 
     def forward_last(c):
-        p, q = c // hz, c % hz
+        p, q = split(c)
 
         @pl.when(jnp.logical_and(relay, my_x % 2 == p))
         def _():
-            arrived(qrecv.at[q], qr.at[q])
-            for e in range(nd):
-                acc = [jnp.zeros((rows, block), f32) for r in range(width)]
-                for n in range(near):
-                    t = qrecv[q, n, e].astype(f32)
-                    v = jnp.broadcast_to(colx[pl.ds(e * nd + source(n), 1), :], (rows, block))
+            for g in range(GROUPS):
+                arrived(qrecv.at[q, g], qr.at[q, g])
+                for e in range(part):
+                    acc = [jnp.zeros((rows, block), f32) for r in range(width)]
+                    for n in range(near):
+                        t = qrecv[q, g, n, e].astype(f32)
+                        v = jnp.broadcast_to(colx[pl.ds((g * part + e) * nd + source(n), 1), :], (rows, block))
+                        for r in range(width):
+                            acc[r] = acc[r] + jnp.where(v == float(r), t, 0.0)
                     for r in range(width):
-                        acc[r] = acc[r] + jnp.where(v == float(r), t, 0.0)
-                for r in range(width):
-                    usend[q, e, r] = acc[r].astype(bf16)
-            remote(usend.at[q], urecv, us, ur, my_x, far_z + q).start()
+                        usend[q, g * part + e, r] = acc[r].astype(bf16)
+                piece = pl.ds(g * part, part)
+                remote(usend.at[q, piece], urecv.at[piece], us, ur.at[g], my_x, (1 - hi) * (hz + q) + hi * (hz - 1 - q)).start()
 
     for c in range(chunks):
         arrived(fin.at[c * per:(c + 1) * per], fr.at[c])
@@ -283,6 +317,7 @@
             send_terms(l + 1, c)
         else:
             send_last(c)
+    release(0)
     for k in range(total - chunks + LAG, total):
         relay_step(k)
 
@@ -296,11 +331,13 @@
                 acc[q] = acc[q] + jnp.where(v == float(q), t, 0.0)
         for q in range(width):
             pre[e * width + q] = acc[q]
-    arrived(urecv, ur)
-    for e in range(nd):
-        for q in range(width):
-            s = (e * width + q) * block
-            out[:, s:s + block] = jnp.maximum(pre[e * width + q] + urecv[e, q].astype(f32), 0.0).astype(bf16)
+    for g in range(GROUPS):
+        piece = urecv.at[g * part:(g + 1) * part]
+        arrived(piece, ur.at[g])
+        for e in range(g * part, (g + 1) * part):
+            for q in range(width):
+                s = (e * width + q) * block
+                out[:, s:s + block] = jnp.maximum(pre[e * width + q] + urecv[e, q].astype(f32), 0.0).astype(bf16)
 
     arrived(fin.at[0:nd - 1], fs)
     arrived(aux.at[0:nd - 1], xs)
@@ -351,8 +388,8 @@
             vmem((nx, steps, hz, size, block), bf16), vmem((steps, near, hz, size, block), bf16), dma, dma, dma((steps,)),
             vmem((steps, hz, width, size, block), bf16), vmem((steps, width, size, block), bf16), dma, dma((steps,)),
             vmem((nd, nd, rows, block), bf16), vmem((near, nd, rows, block), bf16), dma, dma,
-            vmem((hz, near, nd, rows, block), bf16), dma((hz,)),
-            vmem((hz, nd, width, rows, block), bf16), vmem((nd, width, rows, block), bf16), dma, dma,
+            vmem((hz, GROUPS, near, nd // GROUPS, rows, block), bf16), dma((hz, GROUPS)),
+            vmem((hz, nd, width, rows, block), bf16), vmem((nd, width, rows, block), bf16), dma, dma((GROUPS,)),
             vmem((nd * width, rows, block), f32),
         ],
         compiler_params=pltpu.CompilerParams(
@@ -378,7 +415,7 @@
         width = bias.shape[1] // block
         fits = (
             rows % 8 == 0 and nx % 2 == 0 and ny % 2 == 0 and block == 128
-            and nx * ny <= 32 and width + bias.shape[0] <= 8 and (nx * rows) % 16 == 0 and bias.shape[0] > 1
+            and nx * ny <= 32 and nx * ny % GROUPS == 0 and width + bias.shape[0] <= 8 and (nx * rows) % 16 == 0 and bias.shape[0] > 1
         )
         step = functools.partial(fused, nx, ny) if fits else local
         return step(features, link_weight, link_row, link_col, link_live, bias)

time: 41.6 us -> 39.8 us (0.957)
  Pallas kernels: 40.8 us -> 38.8 us
    pallas_call x1, Pallas kernels: 40.8 us -> 38.8 us  [fused(): pl.pallas_call(functools.partial(kernel, nx, ny), out_shape=vmem(features...]
where the time goes in v3:
time: 39.8 us; the launch traced here: 39.5 us
  Pallas kernels  38.8 us (97%)
  local copies, waits for them, and re-layouts  0.66 us (2%)
    pallas_call x1, Pallas kernels, fused(): pl.pallas_call(functools.partial(kernel, nx, ny), out_shape=vmem(features...  38.8 us

profile of v3, /device:TPU:1, one launch (start us, length us, event | category | flops | bytes accessed | tf_op | source)
XLA Modules:
  0.0 39.5 jit_solution(17049190892885293176)
XLA Ops:
  0.0 38.8 %shard_map.64 = bf16[8,8192]{1,0:T(8,128)(2,1)S(1)} custom-call(bf16[8,8192]{1,0:T(8,128)(2,1)} %feat_hbm.1, bf16[3,1,16,128,128]{4,3,2,1,0:T(8,128)(2,1)} %weight_hbm.1, s32[3,1,16]{2,1,0:T(1,128)} %row_hbm.1, s32[3,1,16]{2,1,0:T(1,128)} %bitcast.1, s32[3,1,16]{2,1,0:T(1,128)} %live_hbm.1, f32[3,512]{1,0:T(4,128)} %bias_hbm.1), custom_call_target="tpu_custom_call" | custom-call | tf_op jit(solution)/shard_map/pallas_call | solution.py:375
  38.8 0.7 %copy.8 = bf16[8,8192]{1,0:T(8,128)(2,1)} copy(bf16[8,8192]{1,0:T(8,128)(2,1)S(1)} %shard_map.64) | data formatting | bytes 262144

commit v4 on v3

--- a/solution.py
+++ b/solution.py
@@ -8,7 +8,7 @@
 from jax.sharding import PartitionSpec as P
 
 MESH = pl.DeviceIdType.MESH
-LAG = 2
+LAG = 1
 GROUPS = 4
 DEPTH = 1
 DEPTH_LAST = 1
@@ -78,7 +78,7 @@
     def place(a, b):
         d = (b // hz) * (b - hz) + (1 - b // hz) * (hz - 1 - b)
         p = a % 2
-        return (p * hz + (1 - p) * d + p * (hz - 1 - d)) * per + (a // 2) * 2 + b // hz
+        return ((hz - 1 - d) * 2 + p) * per + (a // 2) * 2 + b // hz
 
     def remote(src, dst, send_sem, recv_sem, a, b):
         return pltpu.make_async_remote_copy(src, dst, send_sem, recv_sem, device_id={"nx": a, "ny": b}, device_id_type=MESH)
@@ -209,8 +209,7 @@
             act[q, c * size:(c + 1) * size, :] = jnp.maximum(acc[q], 0.0).astype(bf16)
 
     def split(c):
-        p = c // hz
-        return p, (1 - p) * (c % hz) + p * (hz - 1 - c % hz)
+        return c % 2, hz - 1 - c // 2
 
     def owners(c):
         p, d = split(c)

time: 39.8 us -> 38.5 us (0.967)
  the two profiles are of different devices: /device:TPU:1 before, /device:TPU:9 now
where the time goes in v4:
time: 38.5 us; the launch traced here: 38.3 us
  Pallas kernels  37.7 us (98%)
  local copies, waits for them, and re-layouts  0.66 us (2%)
    pallas_call x1, Pallas kernels, fused(): pl.pallas_call(functools.partial(kernel, nx, ny), out_shape=vmem(features...  37.7 us

profile of v4, /device:TPU:9, one launch (start us, length us, event | category | flops | bytes accessed | tf_op | source)
XLA Modules:
  0.0 38.3 jit_solution(13851762468974837204)
XLA Ops:
  0.0 37.7 %shard_map.64 = bf16[8,8192]{1,0:T(8,128)(2,1)S(1)} custom-call(bf16[8,8192]{1,0:T(8,128)(2,1)} %feat_hbm.1, bf16[3,1,16,128,128]{4,3,2,1,0:T(8,128)(2,1)} %weight_hbm.1, s32[3,1,16]{2,1,0:T(1,128)} %row_hbm.1, s32[3,1,16]{2,1,0:T(1,128)} %bitcast.1, s32[3,1,16]{2,1,0:T(1,128)} %live_hbm.1, f32[3,512]{1,0:T(4,128)} %bias_hbm.1), custom_call_target="tpu_custom_call" | custom-call | tf_op jit(solution)/shard_map/pallas_call | solution.py:374
  37.7 0.7 %copy.8 = bf16[8,8192]{1,0:T(8,128)(2,1)} copy(bf16[8,8192]{1,0:T(8,128)(2,1)S(1)} %shard_map.64) | data formatting | bytes 262144

commit v5 on v4

--- a/solution.py
+++ b/solution.py
@@ -51,7 +51,7 @@
 
 
 def kernel(nx, ny, feat_hbm, weight_hbm, row_hbm, col_hbm, live_hbm, bias_hbm, out, feat, row, col, live, bias, isem, w, wsem,
-           fin, fs, fr, act, auxs, aux, xs, xr, colx, colr, tsend, trecv, ts, tr, rsend, rrecv, rs, ro, rr, psend, precv, ps, pr,
+           fin, fs, fr, act, cols, bias_out, colg, cs, cr, pair, ns, nr, biasg, bs, br, colx, colr, tsend, trecv, ts, tr, rsend, rrecv, rs, ro, rr, psend, precv, ps, pr,
            lsend, orecv, ls, orr, qrecv, qr, usend, urecv, us, ur, pre):
     nd = nx * ny
     layers = bias.shape[0]
@@ -108,14 +108,14 @@
     for load in loads:
         load.wait()
     lane = lax.broadcasted_iota(jnp.int32, (1, block), 1)
-    auxs[...] = jnp.zeros_like(auxs)
+    cols[...] = jnp.zeros_like(cols)
     for r in range(width):
-        auxs[r:r + 1, :] = bias[layers - 1:layers, r * block:(r + 1) * block]
+        bias_out[r:r + 1, :] = bias[layers - 1:layers, r * block:(r + 1) * block]
     for l in range(layers):
-        cols = jnp.zeros((1, block), jnp.int32)
+        v = jnp.zeros((1, block), jnp.int32)
         for s in range(nd):
-            cols = jnp.where(lane == s, col[l, 0, s], cols)
-        auxs[width + l:width + l + 1, :] = cols.astype(f32)
+            v = jnp.where(lane == s, col[l, 0, s], v)
+        cols[l:l + 1, :] = v.astype(f32)
     pl.semaphore_wait(barrier, nd - 1)
 
     my_place = place(my_x, my_z)
@@ -124,8 +124,11 @@
     for a, b, own in peers:
         at = pl.multiple_of((a * ny + b) * span, span)
         send(feat.at[:, pl.ds(at, span)], fin.at[my_place], fs, fr.at[my_chunk], a, b, own)
+    remote(cols, pair.at[lo], ns, nr, my_x, (1 - hi) * hz + hi * (hz - 1)).start()
     for a, b, own in peers:
-        send(auxs, aux.at[me], xs, xr, a, b, own)
+        send(cols.at[layers - 1:layers], colg.at[pl.ds(me, 1)], cs, cr, a, b, own)
+    for a, b, own in peers:
+        send(bias_out, biasg.at[me], bs, br, a, b, own)
 
     def product(l, c, e):
         x = act[row[l, 0, e], c * size:(c + 1) * size, :]
@@ -282,18 +285,22 @@
             arrived(w.at[0], wsem.at[0])
         send_terms(0, c)
 
-    arrived(aux, xr)
     eye = lax.broadcasted_iota(jnp.int32, (nd, block), 0) == lax.broadcasted_iota(jnp.int32, (nd, block), 1)
     ones = jnp.ones((block, block), bf16)
-    for l in range(layers - 1):
-        for i in range(hz):
-            v = jnp.where(eye, aux[my_x * ny + far_z + i, width + l:width + l + 1, :], 0.0).astype(bf16)
-            m = jnp.dot(v, ones, preferred_element_type=f32)
-            k = (l * hz + i) * nd
-            colr[k:k + nd] = jnp.broadcast_to(m[:, None, :], (nd, 8, block))
+
+    @pl.when(relay)
+    def _():
+        arrived(pair, nr)
+        for l in range(layers - 1):
+            for i in range(hz):
+                v = jnp.where(eye, pair[i, l:l + 1, :], 0.0).astype(bf16)
+                m = jnp.dot(v, ones, preferred_element_type=f32)
+                k = (l * hz + i) * nd
+                colr[k:k + nd] = jnp.broadcast_to(m[:, None, :], (nd, 8, block))
+
+    arrived(colg, cr)
     for e in range(nd):
-        last = width + layers - 1
-        v = jnp.where(eye, aux[e, last:last + 1, :], 0.0).astype(bf16)
+        v = jnp.where(eye, colg[e:e + 1, :], 0.0).astype(bf16)
         colx[e * nd:(e + 1) * nd, :] = jnp.dot(v, ones, preferred_element_type=f32)
 
     total = layers * chunks
@@ -321,8 +328,9 @@
         relay_step(k)
 
     arrived(orecv, orr)
+    arrived(biasg, br)
     for e in range(nd):
-        acc = [jnp.broadcast_to(aux[e, q:q + 1, :], (rows, block)) for q in range(width)]
+        acc = [jnp.broadcast_to(biasg[e, q:q + 1, :], (rows, block)) for q in range(width)]
         for n in range(near):
             t = orecv[n, e].astype(f32)
             v = jnp.broadcast_to(colx[pl.ds(e * nd + source(n), 1), :], (rows, block))
@@ -339,7 +347,9 @@
                 out[:, s:s + block] = jnp.maximum(pre[e * width + q] + urecv[e, q].astype(f32), 0.0).astype(bf16)
 
     arrived(fin.at[0:nd - 1], fs)
-    arrived(aux.at[0:nd - 1], xs)
+    arrived(colg.at[0:nd - 1], cs)
+    arrived(cols, ns)
+    arrived(biasg.at[0:nd - 1], bs)
     arrived(tsend.at[0:near - 1], ts)
     arrived(rsend.at[0:nx - 1], rs)
 
@@ -381,7 +391,8 @@
             vmem((layers, nd, block, block), bf16), dma((layers,)),
             vmem((nd, rows, width * block), bf16), dma, dma((chunks,)),
             vmem((width, rows * nd, block), bf16),
-            vmem((8, block), f32), vmem((nd, 8, block), f32), dma, dma,
+            vmem((8, block), f32), vmem((width, block), f32), vmem((nd, block), f32), dma, dma,
+            vmem((hz, 8, block), f32), dma, dma, vmem((nd, width, block), f32), dma, dma,
             vmem((nd * nd, block), f32), vmem(((layers - 1) * hz * nd, 8, block), f32),
             vmem((near, steps, size, block), bf16), vmem((steps, near, size, block), bf16), dma, dma((steps,)),
             vmem((nx, steps, hz, size, block), bf16), vmem((steps, near, hz, size, block), bf16), dma, dma, dma((steps,)),
@@ -414,7 +425,7 @@
         width = bias.shape[1] // block
         fits = (
             rows % 8 == 0 and nx % 2 == 0 and ny % 2 == 0 and block == 128
-            and nx * ny <= 32 and nx * ny % GROUPS == 0 and width + bias.shape[0] <= 8 and (nx * rows) % 16 == 0 and bias.shape[0] > 1
+            and nx * ny <= 32 and nx * ny % GROUPS == 0 and bias.shape[0] <= 8 and (nx * rows) % 16 == 0 and bias.shape[0] > 1
         )
         step = functools.partial(fused, nx, ny) if fits else local
         return step(features, link_weight, link_row, link_col, link_live, bias)

time: 38.5 us -> 38.1 us (0.990)
  the two profiles are of different devices: /device:TPU:9 before, /device:TPU:1 now
where the time goes in v5:
time: 38.1 us; the launch traced here: 37.5 us
  Pallas kernels  36.9 us (97%)
  local copies, waits for them, and re-layouts  0.66 us (2%)
    pallas_call x1, Pallas kernels, fused(): pl.pallas_call(functools.partial(kernel, nx, ny), out_shape=vmem(features...  36.9 us

profile of v5, /device:TPU:1, one launch (start us, length us, event | category | flops | bytes accessed | tf_op | source)
XLA Modules:
  0.0 37.5 jit_solution(17427176902047423644)
XLA Ops:
  0.0 36.9 %shard_map.64 = bf16[8,8192]{1,0:T(8,128)(2,1)S(1)} custom-call(bf16[8,8192]{1,0:T(8,128)(2,1)} %feat_hbm.1, bf16[3,1,16,128,128]{4,3,2,1,0:T(8,128)(2,1)} %weight_hbm.1, s32[3,1,16]{2,1,0:T(1,128)} %row_hbm.1, s32[3,1,16]{2,1,0:T(1,128)} %bitcast.1, s32[3,1,16]{2,1,0:T(1,128)} %live_hbm.1, f32[3,512]{1,0:T(4,128)} %bias_hbm.1), custom_call_target="tpu_custom_call" | custom-call | tf_op jit(solution)/shard_map/pallas_call | solution.py:384
  36.9 0.7 %copy.8 = bf16[8,8192]{1,0:T(8,128)(2,1)} copy(bf16[8,8192]{1,0:T(8,128)(2,1)S(1)} %shard_map.64) | data formatting | bytes 262144

commit v6 on v5

--- a/solution.py
+++ b/solution.py
@@ -98,14 +98,22 @@
     ]
     for load in loads:
         load.start()
-    for l in range(layers):
-        pltpu.make_async_copy(weight_hbm.at[l, 0], w.at[l], wsem.at[l]).start()
+    pltpu.make_async_copy(weight_hbm.at[:, 0], w, wsem).start()
     barrier = pltpu.get_barrier_semaphore()
     for a, b, own in peers:
         if not own:
             pl.semaphore_signal(barrier, inc=1, device_id={"nx": a, "ny": b}, device_id_type=MESH)
 
-    for load in loads:
+    loads[0].wait()
+    pl.semaphore_wait(barrier, nd - 1)
+
+    my_place = place(my_x, my_z)
+    my_chunk = my_place // per
+    span = width * block
+    for a, b, own in peers:
+        at = pl.multiple_of((a * ny + b) * span, span)
+        send(feat.at[:, pl.ds(at, span)], fin.at[my_place], fs, fr.at[my_chunk], a, b, own)
+    for load in loads[1:]:
         load.wait()
     lane = lax.broadcasted_iota(jnp.int32, (1, block), 1)
     cols[...] = jnp.zeros_like(cols)
@@ -116,14 +124,6 @@
         for s in range(nd):
             v = jnp.where(lane == s, col[l, 0, s], v)
         cols[l:l + 1, :] = v.astype(f32)
-    pl.semaphore_wait(barrier, nd - 1)
-
-    my_place = place(my_x, my_z)
-    my_chunk = my_place // per
-    span = width * block
-    for a, b, own in peers:
-        at = pl.multiple_of((a * ny + b) * span, span)
-        send(feat.at[:, pl.ds(at, span)], fin.at[my_place], fs, fr.at[my_chunk], a, b, own)
     remote(cols, pair.at[lo], ns, nr, my_x, (1 - hi) * hz + hi * (hz - 1)).start()
     for a, b, own in peers:
         send(cols.at[layers - 1:layers], colg.at[pl.ds(me, 1)], cs, cr, a, b, own)
@@ -186,16 +186,17 @@
         def _():
             arrived(rrecv.at[k], rr.at[k])
             for i in range(hz):
+                z = hi * i + (1 - hi) * (hz - 1 - i)
                 acc = [jnp.zeros((size, block), f32) for q in range(width)]
                 for n in range(near):
-                    t = rrecv[k, n, i].astype(f32)
-                    v = colr[pl.ds((l * hz + i) * nd + source(n), 1)][0]
+                    t = rrecv[k, n, z].astype(f32)
+                    v = colr[pl.ds((l * hz + z) * nd + source(n), 1)][0]
                     v = jnp.concatenate([v] * (size // 8), axis=0)
                     for q in range(width):
                         acc[q] = acc[q] + jnp.where(v == float(q), t, 0.0)
                 for q in range(width):
                     psend[k, i, q] = acc[q].astype(bf16)
-                remote(psend.at[k, i], precv.at[k], ps, pr.at[k], my_x, far_z + i).start()
+                remote(psend.at[k, i], precv.at[k], ps, pr.at[k], my_x, far_z + z).start()
 
     def collect(l, c):
         k = l * chunks + c
@@ -282,7 +283,7 @@
             x = fin[c * per:(c + 1) * per, :, r * block:(r + 1) * block].astype(f32).reshape(size, block)
             act[r, c * size:(c + 1) * size, :] = x.astype(bf16)
         if c == 0:
-            arrived(w.at[0], wsem.at[0])
+            arrived(w, wsem)
         send_terms(0, c)
 
     eye = lax.broadcasted_iota(jnp.int32, (nd, block), 0) == lax.broadcasted_iota(jnp.int32, (nd, block), 1)
@@ -317,8 +318,6 @@
         relay_step(k + LAG)
         l, c = k // chunks, k % chunks
         collect(l, c)
-        if c == 0:
-            arrived(w.at[l + 1], wsem.at[l + 1])
         if l + 1 < layers - 1:
             send_terms(l + 1, c)
         else:
@@ -388,7 +387,7 @@
         out_specs=pl.BlockSpec(memory_space=vmem),
         scratch_shapes=[
             vmem(features.shape, bf16), counts, counts, counts, vmem(bias.shape, f32), dma((5,)),
-            vmem((layers, nd, block, block), bf16), dma((layers,)),
+            vmem((layers, nd, block, block), bf16), dma,
             vmem((nd, rows, width * block), bf16), dma, dma((chunks,)),
             vmem((width, rows * nd, block), bf16),
             vmem((8, block), f32), vmem((width, block), f32), vmem((nd, block), f32), dma, dma,

time: 38.1 us -> 38.1 us (level)
  the two profiles are of different devices: /device:TPU:1 before, /device:TPU:0 now
where the time goes in v6:
time: 38.1 us; the launch traced here: 37.9 us
  Pallas kernels  37.3 us (98%)
  local copies, waits for them, and re-layouts  0.66 us (2%)
    pallas_call x1, Pallas kernels, fused(): pl.pallas_call(functools.partial(kernel, nx, ny), out_shape=vmem(features...  37.3 us

profile of v6, /device:TPU:0, one launch (start us, length us, event | category | flops | bytes accessed | tf_op | source)
XLA Modules:
  0.0 37.9 jit_solution(10055580012275004715)
XLA Ops:
  0.0 37.3 %shard_map.64 = bf16[8,8192]{1,0:T(8,128)(2,1)S(1)} custom-call(bf16[8,8192]{1,0:T(8,128)(2,1)} %feat_hbm.1, bf16[3,1,16,128,128]{4,3,2,1,0:T(8,128)(2,1)} %weight_hbm.1, s32[3,1,16]{2,1,0:T(1,128)} %row_hbm.1, s32[3,1,16]{2,1,0:T(1,128)} %bitcast.1, s32[3,1,16]{2,1,0:T(1,128)} %live_hbm.1, f32[3,512]{1,0:T(4,128)} %bias_hbm.1), custom_call_target="tpu_custom_call" | custom-call | tf_op jit(solution)/shard_map/pallas_call | solution.py:383
  37.3 0.7 %copy.8 = bf16[8,8192]{1,0:T(8,128)(2,1)} copy(bf16[8,8192]{1,0:T(8,128)(2,1)S(1)} %shard_map.64) | data formatting | bytes 262144
